TPU v7x, 32 devices: a whole 2x2x4 slice. The times are simulated.
32 devices in a mesh: group: 2 (over y), space: 8 (over z, x), tm: 2 (over core).
Axes of the slice: x: 2, y: 2, z: 4, core: 2. Of those that a mesh axis runs over, the one named last changes fastest.
Arguments:
- w_modes: bfloat16 [12, 1024, 768], P(('group', 'tm'), 'space'), parts along dimension 0, may hold values from -6 to 6
- v_modes: bfloat16 [12, 1024, 768], P(('group', 'tm'), 'space'), parts along dimension 0, may hold values from -6 to 6
- phase_index: int32 [1024], P('space'), may hold values from 0 to 95
- seq_offset: int32 [6], replicated, may hold values from 1 to 5
- owner_block: int32 [8], replicated, may hold values from 0 to 7, each once
Outputs:
- strips: float32 [384, 12, 768], P('space', ('group', 'tm')), parts along dimension 1
- margin: float32 [12, 768], P(('group', 'tm')), parts along dimension 0
There are 2 independent parts, one for each index of `group`. A program takes and returns all parts, laid end to end along the dimension named above; an argument that names none is the same for every part. Nothing has to cross between parts.
Inputs may be any that keep to these rules, and one draw needn't show every extreme that they name: owner_block is a permutation of 0 to 7.
All inputs are finite; a program needn't handle non-finite values.
Results may differ from a plain program's by a relative error of at most 0.0041.
Values may be sent and summed in bfloat16 or wider, within the bound.
No kernel may reach another device: no remote copies, remote signals or barrier semaphores. Data moves between devices by JAX's collectives and lax.ppermute only.
A program may use at most 64 MiB of HBM per device.

v0:
```python
import functools
import math

import jax
import jax.numpy as jnp
from jax import lax
from jax.experimental import pallas as pl
from jax.experimental.pallas import tpu as pltpu
from jax.sharding import PartitionSpec as P


PHASES = 96
LANES = 128
GRANT = 12 * 1024 * 1024


def swap(block, axis, mask):
    size = lax.axis_size(axis)
    return lax.ppermute(block, axis, [(i, i ^ mask) for i in range(size)])


PHASE_ROWS = 16


def prep_kernel(t, nline, block, owner_ref, phase_ref, w_ref, v_ref, send_ref, own_ref, turned):
    width = w_ref.shape[2]
    nmode = width // 2
    me = lax.axis_index("space")
    line, side = me // 2, me % 2
    for c in range(width // LANES):
        turned[c * LANES : (c + 1) * LANES, :] = w_ref[t, :, c * LANES : (c + 1) * LANES].T
    for k in range(nline):
        for half, out_ref in ((1 - side, send_ref), (side, own_ref)):
            rows = owner_ref[2 * (line ^ k) + half] * block
            for part in range(2):
                at = (part * nline + k) * block
                out_ref[at : at + block, :] = turned[pl.ds(pl.multiple_of(part * nmode + rows, block), block), :]
    base, sites = 2 * nline * block, v_ref.shape[1]
    for c in range(width // LANES):
        send_ref[base + c * sites : base + (c + 1) * sites, :] = v_ref[t, :, c * LANES : (c + 1) * LANES]
    base += width // LANES * sites
    phase = phase_ref[...].astype(jnp.float32).astype(jnp.bfloat16)
    send_ref[base : base + PHASE_ROWS, :] = jnp.broadcast_to(phase, (PHASE_ROWS, LANES))


def field_kernel(t, nline, block, scale, phase_ref, v_ref, own_ref, got_ref, *refs):
    (mine_ref, near_ref), far_refs, (left, phased, plain) = refs[:2], refs[2:-3], refs[-3:]
    sites, width = v_ref.shape[1:]
    nmode = width // 2
    rows = nline * block
    base = 2 * rows
    tail = base + width // LANES * sites
    for part in range(2):
        at = 2 * part * sites
        left[:, at : at + sites] = own_ref[part * rows : (part + 1) * rows, :]
        left[:, at + sites : at + 2 * sites] = got_ref[part * rows : (part + 1) * rows, :]
    theirs = got_ref[tail : tail + PHASE_ROWS, :].astype(jnp.float32)[:1]
    angle = jnp.concatenate([phase_ref[...].astype(jnp.float32), theirs], axis=0) * (2.0 * math.pi / PHASES)
    turns = jnp.concatenate([jnp.cos(angle), jnp.sin(angle), jnp.zeros((4, LANES), jnp.float32)], axis=0).T
    for c in range(nmode // LANES):
        re, im = slice(c * LANES, (c + 1) * LANES), slice(nmode + c * LANES, nmode + (c + 1) * LANES)
        far = c + nmode // LANES
        for d in range(2):
            if d == 0:
                vr, vi = v_ref[t, :, re], v_ref[t, :, im]
            else:
                vr = got_ref[base + c * sites : base + (c + 1) * sites, :]
                vi = got_ref[base + far * sites : base + (far + 1) * sites, :]
            top, low = slice(d * sites, (d + 1) * sites), slice((2 + d) * sites, (3 + d) * sites)
            plain[top, re], plain[top, im] = vr, vi
            plain[low, re], plain[low, im] = vi, -vr
            cosv, sinv = turns[:, d : d + 1], turns[:, 2 + d : 3 + d]
            fr, fi = vr.astype(jnp.float32), vi.astype(jnp.float32)
            pr = (cosv * fr + sinv * fi).astype(jnp.bfloat16)
            pi = (cosv * fi - sinv * fr).astype(jnp.bfloat16)
            phased[top, re], phased[top, im] = pr, pi
            phased[low, re], phased[low, im] = pi, -pr

    def part_of(field, k):
        return field[k * block : (k + 1) * block]

    field = jnp.dot(left[...], phased[...], preferred_element_type=jnp.float32) * scale
    mine_ref[0] = part_of(field, 0)
    near_ref[0] = part_of(field, 1).astype(jnp.bfloat16)
    for k in range(2, nline):
        far_refs[k - 2][...] = part_of(field, k).astype(jnp.bfloat16)
    field = jnp.dot(left[...], plain[...], preferred_element_type=jnp.float32) * scale
    for k in range(nline):
        if k % 2 == 0:
            mine_ref[1 + k // 2] = part_of(field, k)
        else:
            near_ref[1 + k // 2] = part_of(field, k).astype(jnp.bfloat16)


def cross_kernel(mine_ref, near_ref, out_ref):
    out_ref[...] = (mine_ref[2] + near_ref[2].astype(jnp.float32)).astype(jnp.bfloat16)


def strip_kernel(tdev, *refs):
    ins, (strip_ref, round_ref) = refs[:-2], refs[-2:]
    each = len(ins) // tdev
    for t in range(tdev):
        mine_ref, near_ref, *far_refs = ins[t * each : (t + 1) * each]
        total = mine_ref[0] + near_ref[0].astype(jnp.float32)
        for far_ref in far_refs:
            total = total + far_ref[...].astype(jnp.float32)
        strip_ref[t] = total
        round_ref[t] = total.astype(jnp.bfloat16)


def margin_kernel(tdev, scale, pick_ref, owner_ref, rounded_ref, other_ref, *refs):
    ins, out_ref = refs[:-1], refs[-1]
    block, width = rounded_ref.shape[1:]
    nmode = width // 2
    first = owner_ref[lax.axis_index("space")] * block
    lane = lax.broadcasted_iota(jnp.int32, (block, nmode), 1)
    row = lax.broadcasted_iota(jnp.int32, (block, nmode), 0)
    here = lane == row + first
    for t in range(tdev):
        mine_ref, near_ref, cross_ref = ins[3 * t : 3 * t + 3]
        total = mine_ref[1] + near_ref[1].astype(jnp.float32) + cross_ref[...].astype(jnp.float32)
        pick = pick_ref[t]
        inside = pick < tdev
        at = jnp.where(inside, pick, pick - tdev)
        matrix = jnp.where(inside, rounded_ref[at], other_ref[at]).astype(jnp.float32)
        mr, mi = matrix[:, :nmode], matrix[:, nmode:]
        gr, gi = total[:, :nmode], total[:, nmode:]
        real = jnp.sum(mr * gr - mi * gi, axis=1, keepdims=True) * scale
        imag = jnp.sum(mr * gi + mi * gr, axis=1, keepdims=True) * scale
        out_ref[t : t + 1, :nmode] = jnp.sum(jnp.where(here, real, 0.0), axis=0, keepdims=True)
        out_ref[t : t + 1, nmode:] = jnp.sum(jnp.where(here, imag, 0.0), axis=0, keepdims=True)


def aligned_shards(w_modes, v_modes, phase_index, seq_offset, owner_block):
    tdev, sdev, width = w_modes.shape
    nmode = width // 2
    nspace, ntm = lax.axis_size("space"), lax.axis_size("tm")
    block, nline = nmode // nspace, nspace // 2
    total_slices = tdev * ntm
    scale_sites = 1.0 / math.sqrt(sdev * nspace)
    scale_modes = 1.0 / math.sqrt(2 * nmode)
    rows = nline * block
    bf16, f32 = jnp.bfloat16, jnp.float32
    vmem, smem = pl.BlockSpec(memory_space=pltpu.VMEM), pl.BlockSpec(memory_space=pltpu.SMEM)
    shape = jax.ShapeDtypeStruct

    def call(kernel, outs, n_scalar, cost, args, scratch=()):
        return pl.pallas_call(
            kernel,
            out_shape=outs,
            in_specs=[smem] * n_scalar + [vmem] * (len(args) - n_scalar),
            out_specs=jax.tree.map(lambda _: vmem, outs),
            scratch_shapes=scratch,
            compiler_params=pltpu.CompilerParams(vmem_limit_bytes=GRANT),
            cost_estimate=pl.CostEstimate(flops=cost, bytes_accessed=1_000_000, transcendentals=0),
        )(*args)

    phases = phase_index.reshape(1, sdev)
    packed = 2 * rows + width // LANES * sdev + PHASE_ROWS
    sends, owns = [], []
    for t in range(tdev):
        send, own = call(
            functools.partial(prep_kernel, t, nline, block),
            (shape((packed, LANES), bf16), shape((2 * rows, LANES), bf16)),
            1,
            4_000_000,
            (owner_block, phases, w_modes, v_modes),
            [pltpu.VMEM((width, LANES), bf16)],
        )
        sends.append(send)
        owns.append(own)
    gots = [swap(send, "space", 1) for send in sends]

    fields, sums = [], []
    for t in range(tdev):
        mine, near, *fars = call(
            functools.partial(field_kernel, t, nline, block, scale_sites),
            [shape((3, block, width), f32), shape((3, block, width), bf16)] + [shape((block, width), bf16)] * (nline - 2),
            0,
            4 * rows * 4 * sdev * width,
            (phases, v_modes, owns[t], gots[t]),
            [pltpu.VMEM((rows, 4 * sdev), bf16)] + [pltpu.VMEM((4 * sdev, width), bf16)] * 2,
        )
        near = swap(near, "space", 2)
        fars = [swap(far, "space", 2 * k) for k, far in enumerate(fars, 2)]
        cross = call(cross_kernel, shape((block, width), bf16), 0, 1_000_000, (mine, near))
        fields.extend([mine, near, *fars])
        sums.extend([mine, near, swap(cross, "space", 4)])

    strips, rounded = call(
        functools.partial(strip_kernel, tdev),
        (shape((tdev, block, width), f32), shape((tdev, block, width), bf16)),
        0,
        1_000_000,
        fields,
    )
    other = swap(rounded, "tm", 1)

    rank = lax.axis_index("tm")
    global_slice = rank * tdev + jnp.arange(tdev, dtype=jnp.int32)
    target = (global_slice + jnp.take(seq_offset, global_slice)) % total_slices
    pick = (target - rank * tdev) % total_slices
    margin = call(
        functools.partial(margin_kernel, tdev, scale_modes),
        shape((tdev, width), f32),
        2,
        1_000_000,
        (pick, owner_block, rounded, other, *sums),
    )
    mask = 1
    while mask < nspace:
        margin = margin + swap(margin, "space", mask)
        mask *= 2
    return jnp.transpose(strips, (1, 0, 2)), margin


def general_shards(w_modes, v_modes, phase_index, seq_offset, owner_block):
    tdev, sdev, width = w_modes.shape
    nmode = width // 2
    nspace = lax.axis_size("space")
    ntm = lax.axis_size("tm")
    block = nmode // nspace
    total_slices = tdev * ntm
    scale_sites = 1.0 / math.sqrt(sdev * nspace)
    scale_modes = 1.0 / math.sqrt(2 * nmode)
    order = (owner_block[:, None] * block + jnp.arange(block, dtype=jnp.int32)[None, :]).reshape(-1)
    w_real = jnp.take(w_modes[:, :, :nmode], order, axis=2)
    w_imag = jnp.take(w_modes[:, :, nmode:], order, axis=2)
    left = jnp.concatenate([w_real, w_imag], axis=1)
    angle = phase_index.astype(jnp.float32) * (2.0 * math.pi / PHASES)
    cosv = jnp.cos(angle)[None, :, None]
    sinv = jnp.sin(angle)[None, :, None]
    v_real = v_modes[:, :, :nmode].astype(jnp.float32)
    v_imag = v_modes[:, :, nmode:].astype(jnp.float32)
    ph_real = (cosv * v_real + sinv * v_imag).astype(jnp.bfloat16)
    ph_imag = (cosv * v_imag - sinv * v_real).astype(jnp.bfloat16)
    right = jnp.concatenate(
        [jnp.concatenate([ph_real, ph_imag], axis=2), jnp.concatenate([ph_imag, -ph_real], axis=2)],
        axis=1,
    )
    rank = lax.axis_index("tm")
    global_slice = rank * tdev + jnp.arange(tdev, dtype=jnp.int32)
    target = (global_slice + jnp.take(seq_offset, global_slice)) % total_slices
    pick = (target - rank * tdev) % total_slices
    v_two = jnp.concatenate(
        [
            jnp.concatenate([v_modes[:, :, :nmode], -v_modes[:, :, nmode:]], axis=2),
            jnp.concatenate([v_modes[:, :, nmode:], v_modes[:, :, :nmode]], axis=2),
        ],
        axis=1,
    )
    full = lax.psum(
        jnp.einsum("tsi,tsj->itj", left, right, preferred_element_type=jnp.float32) * scale_sites,
        "space",
    )
    strips = lax.dynamic_slice_in_dim(full, lax.axis_index("space") * block, block, 0)
    rounded = full.astype(jnp.bfloat16)
    pieces = [rounded]
    for step in range(1, ntm):
        route = [((i + step) % ntm, i) for i in range(ntm)]
        pieces.append(lax.ppermute(rounded, "tm", route))
    chosen = jnp.take(jnp.concatenate(pieces, axis=1), pick, axis=1)
    seq_raw = jnp.einsum("tsj,itj->tsi", v_two, chosen, preferred_element_type=jnp.float32)
    seq = seq_raw * scale_modes
    seq_real = seq[:, :sdev]
    seq_imag = seq[:, sdev:]
    wr_full = w_real.astype(jnp.float32)
    wi_full = w_imag.astype(jnp.float32)
    over_real = jnp.sum(wr_full * seq_real + wi_full * seq_imag, axis=1) * scale_sites
    over_imag = jnp.sum(wr_full * seq_imag - wi_full * seq_real, axis=1) * scale_sites
    total_real, total_imag = lax.psum((over_real, over_imag), "space")
    margin = jnp.zeros((tdev, 2 * nmode), jnp.float32)
    margin = margin.at[:, order].set(total_real).at[:, order + nmode].set(total_imag)
    return (strips, margin)


def shards(w_modes, v_modes, phase_index, seq_offset, owner_block):
    _, sdev, width = w_modes.shape
    nmode, nspace = width // 2, lax.axis_size("space")
    square = nspace == 2 * 4
    tiles = nmode % (nspace * 16) == 0 and nmode % LANES == 0 and sdev == LANES
    body = aligned_shards if square and tiles and lax.axis_size("tm") == 2 else general_shards
    return body(w_modes, v_modes, phase_index, seq_offset, owner_block)


def solution(mesh):
    in_specs = (
        P(("group", "tm"), "space", None),
        P(("group", "tm"), "space", None),
        P("space"),
        P(),
        P(),
    )
    out_specs = (P("space", ("group", "tm"), None), P(("group", "tm"), None))
    step = jax.shard_map(shards, mesh=mesh, in_specs=in_specs, out_specs=out_specs, check_vma=False)

    def run(w_modes, *rest):
        return step(w_modes, *rest)

    return run if mesh.shape["space"] == 8 else step
```

profile of v0, /device:TPU:0, one launch (start us, length us, event | category | flops | bytes accessed | tf_op | source)
XLA Modules:
  0.0 77.1 jit_solution(11735698297267423249)
XLA Ops:
  0.6 0.0 copy-start
  0.7 0.6 copy-done.5
  1.3 0.0 copy-done.4
  1.3 1.1 %copy-done.1 = bf16[3,128,768]{2,1,0:T(8,128)(2,1)S(1)} copy-done((bf16[3,128,768]{2,1,0:T(8,128)(2,1)S(1)}, bf16[3,128,768]{2,1,0:T(8,128)(2,1)}, u32[]{:S(2)}) %copy-start.1) | copy-done | bytes 589848
  2.4 1.1 %copy-done.2 = bf16[3,128,768]{2,1,0:T(8,128)(2,1)S(1)} copy-done((bf16[3,128,768]{2,1,0:T(8,128)(2,1)S(1)}, bf16[3,128,768]{2,1,0:T(8,128)(2,1)}, u32[]{:S(2)}) %copy-start.2) | copy-done | bytes 589848
  3.5 0.7 shard_map.72
  4.1 3.0 %collective-permute-start.8 = (bf16[1168,128]{1,0:T(8,128)(2,1)S(1)}, bf16[1168,128]{1,0:T(8,128)(2,1)S(1)}, u32[]{:S(2)}, u32[]{:S(2)}) collective-permute-start(bf16[1168,128]{1,0:T(8,128)(2,1)S(1)} %get-tuple-element.35), channel_id=1, source_target_pairs={{0,2},{2,0},{4,6},{6,4},{8,10},{10,8},{12,14},{14,12},{1,3},{3,1},... | collective-permute-start | bytes 897032 | tf_op jit(solution)/shard_map/ppermute | solution.py:19
  7.1 0.7 shard_map.70
  7.8 0.0 copy-start.3
  7.8 0.1 collective-permute-start.4
  7.9 0.7 shard_map.68
  8.6 0.0 copy-start.6
  8.6 2.1 %collective-permute-start = (bf16[1168,128]{1,0:T(8,128)(2,1)S(1)}, bf16[1168,128]{1,0:T(8,128)(2,1)S(1)}, u32[]{:S(2)}, u32[]{:S(2)}) collective-permute-start(bf16[1168,128]{1,0:T(8,128)(2,1)S(1)} %get-tuple-element.23), channel_id=1, source_target_pairs={{0,2},{2,0},{4,6},{6,4},{8,10},{10,8},{12,14},{14,12},{1,3},{3,1},... | collective-permute-start | bytes 897032 | tf_op jit(solution)/shard_map/ppermute | solution.py:19
  10.7 4.4 %collective-permute-done.8.got_ref = bf16[1168,128]{1,0:T(8,128)(2,1)S(1)} collective-permute-done((bf16[1168,128]{1,0:T(8,128)(2,1)S(1)}, bf16[1168,128]{1,0:T(8,128)(2,1)S(1)}, u32[]{:S(2)}, u32[]{:S(2)}) %collective-permute-start.8) | collective-permute-done | bytes 299040 | tf_op jit(solution)/shard_map/ppermute | solution.py:19
  15.1 1.4 %shard_map.73 = (f32[3,48,768]{2,1,0:T(8,128)S(1)}, bf16[3,48,768]{2,1,0:T(8,128)(2,1)S(1)}, bf16[48,768]{1,0:T(8,128)(2,1)}, bf16[48,768]{1,0:T(8,128)(2,1)S(1)}) custom-call(s32[1,128]{1,0:T(1,128)S(1)} %bitcast.7, bf16[3,128,768]{2,1,0:T(8,128)(2,1)S(1)} %copy-done.3, bf16[384,128]{1,0:T(8,128)(2,1)S(1)} %get-tuple-element.34.own_ref, ...), custom_call_target="tpu_custom_call" | custom-call | flops 301989888 | bytes 1000000 | tf_op jit(solution)/shard_map/pallas_call | solution.py:148
  16.5 3.1 %collective-permute-start.10 = (bf16[48,768]{1,0:T(8,128)(2,1)}, bf16[48,768]{1,0:T(8,128)(2,1)S(1)}, u32[]{:S(2)}, u32[]{:S(2)}) collective-permute-start(bf16[48,768]{1,0:T(8,128)(2,1)} %get-tuple-element.38), channel_id=1, source_target_pairs={{0,8},{2,10},{4,12},{6,14},{8,0},{10,2},{12,4},{14,6},{1,9},{3,11}... | collective-permute-start | bytes 221192 | tf_op jit(solution)/shard_map/ppermute | solution.py:19
  19.6 1.4 %collective-permute-start.11 = (bf16[48,768]{1,0:T(8,128)(2,1)S(1)}, bf16[48,768]{1,0:T(8,128)(2,1)S(1)}, u32[]{:S(2)}, u32[]{:S(2)}) collective-permute-start(bf16[48,768]{1,0:T(8,128)(2,1)S(1)} %get-tuple-element.39), channel_id=1, source_target_pairs={{0,12},{2,14},{4,8},{6,10},{8,4},{10,6},{12,0},{14,2},{1,13},{3,15... | collective-permute-start | bytes 221192 | tf_op jit(solution)/shard_map/ppermute | solution.py:19
  20.9 0.6 collective-permute-done.4.got_ref
  21.5 0.9 %shard_map.71 = (f32[3,48,768]{2,1,0:T(8,128)S(1)}, bf16[3,48,768]{2,1,0:T(8,128)(2,1)S(1)}, bf16[48,768]{1,0:T(8,128)(2,1)S(1)}, bf16[48,768]{1,0:T(8,128)(2,1)S(1)}) custom-call(s32[1,128]{1,0:T(1,128)S(1)} %bitcast.8, bf16[3,128,768]{2,1,0:T(8,128)(2,1)S(1)} %copy-done.3, bf16[384,128]{1,0:T(8,128)(2,1)S(1)} %get-tuple-element.28.own_ref, ...), custom_call_target="tpu_custom_call" | custom-call | flops 301989888 | bytes 1000000 | tf_op jit(solution)/shard_map/pallas_call | solution.py:148
  22.4 2.2 %collective-permute-start.5 = (bf16[3,48,768]{2,1,0:T(8,128)(2,1)S(1)}, bf16[3,48,768]{2,1,0:T(8,128)(2,1)S(1)}, u32[]{:S(2)}, u32[]{:S(2)}) collective-permute-start(bf16[3,48,768]{2,1,0:T(8,128)(2,1)S(1)} %get-tuple-element.31), channel_id=1, source_target_pairs={{0,4},{2,6},{4,0},{6,2},{8,12},{10,14},{12,8},{14,10},{1,5},{3,7},... | collective-permute-start | bytes 663560 | tf_op jit(solution)/shard_map/ppermute | solution.py:19
  24.5 0.1 collective-permute-start.9
  24.6 2.4 %collective-permute-done.got_ref = bf16[1168,128]{1,0:T(8,128)(2,1)S(1)} collective-permute-done((bf16[1168,128]{1,0:T(8,128)(2,1)S(1)}, bf16[1168,128]{1,0:T(8,128)(2,1)S(1)}, u32[]{:S(2)}, u32[]{:S(2)}) %collective-permute-start) | collective-permute-done | bytes 299040 | tf_op jit(solution)/shard_map/ppermute | solution.py:19
  27.1 1.4 %shard_map.69 = (f32[3,48,768]{2,1,0:T(8,128)S(1)}, bf16[3,48,768]{2,1,0:T(8,128)(2,1)S(1)}, bf16[48,768]{1,0:T(8,128)(2,1)}, bf16[48,768]{1,0:T(8,128)(2,1)}) custom-call(s32[1,128]{1,0:T(1,128)S(1)} %bitcast.9, bf16[3,128,768]{2,1,0:T(8,128)(2,1)S(1)} %copy-done.3, bf16[384,128]{1,0:T(8,128)(2,1)S(1)} %copy-done.7, ...), custom_call_target="tpu_custom_call" | custom-call | flops 301989888 | bytes 1000000 | tf_op jit(solution)/shard_map/pallas_call | solution.py:148
  28.5 1.8 %collective-permute-start.1 = (bf16[3,48,768]{2,1,0:T(8,128)(2,1)S(1)}, bf16[3,48,768]{2,1,0:T(8,128)(2,1)S(1)}, u32[]{:S(2)}, u32[]{:S(2)}) collective-permute-start(bf16[3,48,768]{2,1,0:T(8,128)(2,1)S(1)} %get-tuple-element.25), channel_id=1, source_target_pairs={{0,4},{2,6},{4,0},{6,2},{8,12},{10,14},{12,8},{14,10},{1,5},{3,7},... | collective-permute-start | bytes 663560 | tf_op jit(solution)/shard_map/ppermute | solution.py:19
  30.3 0.0 collective-permute-done.10.refs_10_
  30.3 2.6 %collective-permute-start.6 = (bf16[48,768]{1,0:T(8,128)(2,1)S(1)}, bf16[48,768]{1,0:T(8,128)(2,1)S(1)}, u32[]{:S(2)}, u32[]{:S(2)}) collective-permute-start(bf16[48,768]{1,0:T(8,128)(2,1)S(1)} %get-tuple-element.32), channel_id=1, source_target_pairs={{0,8},{2,10},{4,12},{6,14},{8,0},{10,2},{12,4},{14,6},{1,9},{3,11}... | collective-permute-start | bytes 221192 | tf_op jit(solution)/shard_map/ppermute | solution.py:19
  32.9 0.0 collective-permute-done.11.refs_11_
  32.9 6.5 %collective-permute-done.6.refs_6_ = bf16[48,768]{1,0:T(8,128)(2,1)S(1)} collective-permute-done((bf16[48,768]{1,0:T(8,128)(2,1)S(1)}, bf16[48,768]{1,0:T(8,128)(2,1)S(1)}, u32[]{:S(2)}, u32[]{:S(2)}) %collective-permute-start.6) | collective-permute-done | bytes 73760 | tf_op jit(solution)/shard_map/ppermute | solution.py:19
  39.4 3.6 %collective-permute-start.2 = (bf16[48,768]{1,0:T(8,128)(2,1)}, bf16[48,768]{1,0:T(8,128)(2,1)S(1)}, u32[]{:S(2)}, u32[]{:S(2)}) collective-permute-start(bf16[48,768]{1,0:T(8,128)(2,1)} %get-tuple-element.26), channel_id=1, source_target_pairs={{0,8},{2,10},{4,12},{6,14},{8,0},{10,2},{12,4},{14,6},{1,9},{3,11}... | collective-permute-start | bytes 221192 | tf_op jit(solution)/shard_map/ppermute | solution.py:19
  43.0 1.1 %collective-permute-done.7.refs_7_ = bf16[48,768]{1,0:T(8,128)(2,1)S(1)} collective-permute-done((bf16[48,768]{1,0:T(8,128)(2,1)S(1)}, bf16[48,768]{1,0:T(8,128)(2,1)S(1)}, u32[]{:S(2)}, u32[]{:S(2)}) %collective-permute-start.7) | collective-permute-done | bytes 73760 | tf_op jit(solution)/shard_map/ppermute | solution.py:19
  44.0 1.4 %collective-permute-start.3 = (bf16[48,768]{1,0:T(8,128)(2,1)}, bf16[48,768]{1,0:T(8,128)(2,1)S(1)}, u32[]{:S(2)}, u32[]{:S(2)}) collective-permute-start(bf16[48,768]{1,0:T(8,128)(2,1)} %get-tuple-element.27), channel_id=1, source_target_pairs={{0,12},{2,14},{4,8},{6,10},{8,4},{10,6},{12,0},{14,2},{1,13},{3,15... | collective-permute-start | bytes 221192 | tf_op jit(solution)/shard_map/ppermute | solution.py:19
  45.5 0.6 gather_fusion
  46.1 0.2 collective-permute-done.2.refs_2_
  46.3 4.1 %collective-permute-done.3.refs_3_ = bf16[48,768]{1,0:T(8,128)(2,1)S(1)} collective-permute-done((bf16[48,768]{1,0:T(8,128)(2,1)}, bf16[48,768]{1,0:T(8,128)(2,1)S(1)}, u32[]{:S(2)}, u32[]{:S(2)}) %collective-permute-start.3) | collective-permute-done | bytes 73760 | tf_op jit(solution)/shard_map/ppermute | solution.py:19
  50.4 0.9 %shard_map.74 = (f32[3,48,768]{2,1,0:T(8,128)}, bf16[3,48,768]{2,1,0:T(8,128)(2,1)S(1)}) custom-call(f32[3,48,768]{2,1,0:T(8,128)S(1)} %get-tuple-element.24.refs_0_.mine_ref, bf16[3,48,768]{2,1,0:T(8,128)(2,1)S(1)} %collective-permute-done.1.refs_1_.near_ref, bf16[48,768]{1,0:T(8,128)(2,1)S(1)} %collective-permute-done.2.refs_2_, ...), custom_call_target="tpu_custom_call" | custom-call | flops 1000000 | bytes 1000000 | tf_op jit(solution)/shard_map/pallas_call | solution.py:148
  51.3 0.1 collective-permute-start.14
  51.4 3.0 %collective-permute-start.15 = (bf16[48,768]{1,0:T(8,128)(2,1)S(1)}, bf16[48,768]{1,0:T(8,128)(2,1)S(1)}, u32[]{:S(2)}, u32[]{:S(2)}) collective-permute-start(bf16[48,768]{1,0:T(8,128)(2,1)S(1)} %shard_map.77), channel_id=1, source_target_pairs={{0,8},{2,10},{4,12},{6,14},{8,0},{10,2},{12,4},{14,6},{1,9},{3,11}... | collective-permute-start | bytes 221192 | tf_op jit(solution)/shard_map/ppermute | solution.py:19
  54.4 0.1 collective-permute-start.13
  54.5 6.1 %collective-permute-done.14.refs_5_ = bf16[48,768]{1,0:T(8,128)(2,1)S(1)} collective-permute-done((bf16[48,768]{1,0:T(8,128)(2,1)S(1)}, bf16[48,768]{1,0:T(8,128)(2,1)S(1)}, u32[]{:S(2)}, u32[]{:S(2)}) %collective-permute-start.14) | collective-permute-done | bytes 73760 | tf_op jit(solution)/shard_map/ppermute | solution.py:19
  60.6 1.6 %collective-permute-done.15.refs_8_ = bf16[48,768]{1,0:T(8,128)(2,1)S(1)} collective-permute-done((bf16[48,768]{1,0:T(8,128)(2,1)S(1)}, bf16[48,768]{1,0:T(8,128)(2,1)S(1)}, u32[]{:S(2)}, u32[]{:S(2)}) %collective-permute-start.15) | collective-permute-done | bytes 73760 | tf_op jit(solution)/shard_map/ppermute | solution.py:19
  62.1 1.5 %collective-permute-done.13.refs_2_ = bf16[48,768]{1,0:T(8,128)(2,1)S(1)} collective-permute-done((bf16[48,768]{1,0:T(8,128)(2,1)S(1)}, bf16[48,768]{1,0:T(8,128)(2,1)S(1)}, u32[]{:S(2)}, u32[]{:S(2)}) %collective-permute-start.13) | collective-permute-done | bytes 73760 | tf_op jit(solution)/shard_map/ppermute | solution.py:19
  63.6 0.8 %shard_map.78 = f32[3,768]{1,0:T(4,128)S(1)} custom-call(s32[3]{0:T(128)S(1)} %and_select_fusion.pick_ref, s32[8]{0:T(128)S(1)} %copy-done.4, bf16[3,48,768]{2,1,0:T(8,128)(2,1)S(1)} %get-tuple-element.41.rounded_ref, bf16[3,48,768]{2,1,0:T(8,128)(2,1)S(1)} %collective-permute-done.12.other_ref, f32[3,48,768]{2,1,0:T(8,128)S(1)} %get-tuple-element.24.refs_0_.mine_ref, ...), custom_call_target="tpu_custom_call" | custom-call | flops 1000000 | bytes 1000000 | tf_op jit(solution)/shard_map/pallas_call | solution.py:148
  64.4 1.6 %collective-permute-start.16 = (f32[3,768]{1,0:T(4,128)S(1)}, f32[3,768]{1,0:T(4,128)S(1)}, u32[]{:S(2)}, u32[]{:S(2)}) collective-permute-start(f32[3,768]{1,0:T(4,128)S(1)} %shard_map.78), channel_id=1, source_target_pairs={{0,2},{2,0},{4,6},{6,4},{8,10},{10,8},{12,14},{14,12},{1,3},{3,1},... | collective-permute-start | bytes 27656 | tf_op jit(solution)/shard_map/ppermute | solution.py:19
  66.0 2.2 %collective-permute-done.16 = f32[3,768]{1,0:T(4,128)S(1)} collective-permute-done((f32[3,768]{1,0:T(4,128)S(1)}, f32[3,768]{1,0:T(4,128)S(1)}, u32[]{:S(2)}, u32[]{:S(2)}) %collective-permute-start.16) | collective-permute-done | bytes 9248 | tf_op jit(solution)/shard_map/ppermute | solution.py:19
  68.2 3.7 %collective-permute-done.17 = f32[3,768]{1,0:T(4,128)S(1)} collective-permute-done((f32[3,768]{1,0:T(4,128)S(1)}, f32[3,768]{1,0:T(4,128)S(1)}, u32[]{:S(2)}, u32[]{:S(2)}) %collective-permute-start.17) | collective-permute-done | bytes 9248 | tf_op jit(solution)/shard_map/ppermute | solution.py:19
  71.9 0.9 %collective-permute-start.18 = (f32[3,768]{1,0:T(4,128)S(1)}, f32[3,768]{1,0:T(4,128)S(1)}, u32[]{:S(2)}, u32[]{:S(2)}) collective-permute-start(f32[3,768]{1,0:T(4,128)S(1)} %add.66), channel_id=1, source_target_pairs={{0,8},{2,10},{4,12},{6,14},{8,0},{10,2},{12,4},{14,6},{1,9},{3,11}... | collective-permute-start | bytes 27656 | tf_op jit(solution)/shard_map/ppermute | solution.py:19
  72.8 3.7 %collective-permute-done.18 = f32[3,768]{1,0:T(4,128)S(1)} collective-permute-done((f32[3,768]{1,0:T(4,128)S(1)}, f32[3,768]{1,0:T(4,128)S(1)}, u32[]{:S(2)}, u32[]{:S(2)}) %collective-permute-start.18) | collective-permute-done | bytes 9248 | tf_op jit(solution)/shard_map/ppermute | solution.py:19
  76.5 0.6 add.67
  (24 shorter events, 0.1 us)
Async XLA Ops:
  0.6 44.8 %copy-start = (s32[6]{0:T(128)S(1)}, s32[6]{0:T(128)}, u32[]{:S(2)}) copy-start(s32[6]{0:T(128)} %param.8) | copy-start | bytes 76
  0.6 0.7 copy-start.5
  0.7 0.7 copy-start.4
  1.3 1.1 %copy-start.1 = (bf16[3,128,768]{2,1,0:T(8,128)(2,1)S(1)}, bf16[3,128,768]{2,1,0:T(8,128)(2,1)}, u32[]{:S(2)}) copy-start(bf16[3,128,768]{2,1,0:T(8,128)(2,1)} %w_ref.5) | copy-start | bytes 1769476
  2.4 1.1 %copy-start.2 = (bf16[3,128,768]{2,1,0:T(8,128)(2,1)S(1)}, bf16[3,128,768]{2,1,0:T(8,128)(2,1)}, u32[]{:S(2)}) copy-start(bf16[3,128,768]{2,1,0:T(8,128)(2,1)} %v_ref.11) | copy-start | bytes 1769476
  4.1 11.0 %collective-permute-start.8 = (bf16[1168,128]{1,0:T(8,128)(2,1)S(1)}, bf16[1168,128]{1,0:T(8,128)(2,1)S(1)}, u32[]{:S(2)}, u32[]{:S(2)}) collective-permute-start(bf16[1168,128]{1,0:T(8,128)(2,1)S(1)} %get-tuple-element.35), channel_id=1, source_target_pairs={{0,2},{2,0},{4,6},{6,4},{8,10},{10,8},{12,14},{14,12},{1,3},{3,1},... | collective-permute-start | bytes 897032 | tf_op jit(solution)/shard_map/ppermute | solution.py:19
  7.8 7.3 %copy-start.3 = (bf16[3,128,768]{2,1,0:T(8,128)(2,1)S(1)}, bf16[3,128,768]{2,1,0:T(8,128)(2,1)}, u32[]{:S(2)}) copy-start(bf16[3,128,768]{2,1,0:T(8,128)(2,1)} %v_ref.11) | copy-start | bytes 1769476
  7.8 13.7 %collective-permute-start.4 = (bf16[1168,128]{1,0:T(8,128)(2,1)S(1)}, bf16[1168,128]{1,0:T(8,128)(2,1)S(1)}, u32[]{:S(2)}, u32[]{:S(2)}) collective-permute-start(bf16[1168,128]{1,0:T(8,128)(2,1)S(1)} %get-tuple-element.29), channel_id=1, source_target_pairs={{0,2},{2,0},{4,6},{6,4},{8,10},{10,8},{12,14},{14,12},{1,3},{3,1},... | collective-permute-start | bytes 897032 | tf_op jit(solution)/shard_map/ppermute | solution.py:19
  8.6 7.9 %copy-start.6 = (bf16[384,128]{1,0:T(8,128)(2,1)}, bf16[384,128]{1,0:T(8,128)(2,1)S(1)}, u32[]{:S(2)}) copy-start(bf16[384,128]{1,0:T(8,128)(2,1)S(1)} %get-tuple-element.22.own_ref) | copy-start | bytes 294916
  8.6 18.5 %collective-permute-start = (bf16[1168,128]{1,0:T(8,128)(2,1)S(1)}, bf16[1168,128]{1,0:T(8,128)(2,1)S(1)}, u32[]{:S(2)}, u32[]{:S(2)}) collective-permute-start(bf16[1168,128]{1,0:T(8,128)(2,1)S(1)} %get-tuple-element.23), channel_id=1, source_target_pairs={{0,2},{2,0},{4,6},{6,4},{8,10},{10,8},{12,14},{14,12},{1,3},{3,1},... | collective-permute-start | bytes 897032 | tf_op jit(solution)/shard_map/ppermute | solution.py:19
  16.5 13.8 %collective-permute-start.10 = (bf16[48,768]{1,0:T(8,128)(2,1)}, bf16[48,768]{1,0:T(8,128)(2,1)S(1)}, u32[]{:S(2)}, u32[]{:S(2)}) collective-permute-start(bf16[48,768]{1,0:T(8,128)(2,1)} %get-tuple-element.38), channel_id=1, source_target_pairs={{0,8},{2,10},{4,12},{6,14},{8,0},{10,2},{12,4},{14,6},{1,9},{3,11}... | collective-permute-start | bytes 221192 | tf_op jit(solution)/shard_map/ppermute | solution.py:19
  19.6 13.3 %collective-permute-start.11 = (bf16[48,768]{1,0:T(8,128)(2,1)S(1)}, bf16[48,768]{1,0:T(8,128)(2,1)S(1)}, u32[]{:S(2)}, u32[]{:S(2)}) collective-permute-start(bf16[48,768]{1,0:T(8,128)(2,1)S(1)} %get-tuple-element.39), channel_id=1, source_target_pairs={{0,12},{2,14},{4,8},{6,10},{8,4},{10,6},{12,0},{14,2},{1,13},{3,15... | collective-permute-start | bytes 221192 | tf_op jit(solution)/shard_map/ppermute | solution.py:19
  21.5 5.6 %copy-start.7 = (bf16[384,128]{1,0:T(8,128)(2,1)S(1)}, bf16[384,128]{1,0:T(8,128)(2,1)}, u32[]{:S(2)}) copy-start(bf16[384,128]{1,0:T(8,128)(2,1)} %copy-done.6) | copy-start | bytes 294916
  22.4 28.0 %collective-permute-start.5 = (bf16[3,48,768]{2,1,0:T(8,128)(2,1)S(1)}, bf16[3,48,768]{2,1,0:T(8,128)(2,1)S(1)}, u32[]{:S(2)}, u32[]{:S(2)}) collective-permute-start(bf16[3,48,768]{2,1,0:T(8,128)(2,1)S(1)} %get-tuple-element.31), channel_id=1, source_target_pairs={{0,4},{2,6},{4,0},{6,2},{8,12},{10,14},{12,8},{14,10},{1,5},{3,7},... | collective-permute-start | bytes 663560 | tf_op jit(solution)/shard_map/ppermute | solution.py:19
  24.5 25.8 %collective-permute-start.9 = (bf16[3,48,768]{2,1,0:T(8,128)(2,1)S(1)}, bf16[3,48,768]{2,1,0:T(8,128)(2,1)S(1)}, u32[]{:S(2)}, u32[]{:S(2)}) collective-permute-start(bf16[3,48,768]{2,1,0:T(8,128)(2,1)S(1)} %get-tuple-element.37), channel_id=1, source_target_pairs={{0,4},{2,6},{4,0},{6,2},{8,12},{10,14},{12,8},{14,10},{1,5},{3,7},... | collective-permute-start | bytes 663560 | tf_op jit(solution)/shard_map/ppermute | solution.py:19
  28.5 21.9 %collective-permute-start.1 = (bf16[3,48,768]{2,1,0:T(8,128)(2,1)S(1)}, bf16[3,48,768]{2,1,0:T(8,128)(2,1)S(1)}, u32[]{:S(2)}, u32[]{:S(2)}) collective-permute-start(bf16[3,48,768]{2,1,0:T(8,128)(2,1)S(1)} %get-tuple-element.25), channel_id=1, source_target_pairs={{0,4},{2,6},{4,0},{6,2},{8,12},{10,14},{12,8},{14,10},{1,5},{3,7},... | collective-permute-start | bytes 663560 | tf_op jit(solution)/shard_map/ppermute | solution.py:19
  30.3 9.1 %collective-permute-start.6 = (bf16[48,768]{1,0:T(8,128)(2,1)S(1)}, bf16[48,768]{1,0:T(8,128)(2,1)S(1)}, u32[]{:S(2)}, u32[]{:S(2)}) collective-permute-start(bf16[48,768]{1,0:T(8,128)(2,1)S(1)} %get-tuple-element.32), channel_id=1, source_target_pairs={{0,8},{2,10},{4,12},{6,14},{8,0},{10,2},{12,4},{14,6},{1,9},{3,11}... | collective-permute-start | bytes 221192 | tf_op jit(solution)/shard_map/ppermute | solution.py:19
  32.9 11.1 %collective-permute-start.7 = (bf16[48,768]{1,0:T(8,128)(2,1)S(1)}, bf16[48,768]{1,0:T(8,128)(2,1)S(1)}, u32[]{:S(2)}, u32[]{:S(2)}) collective-permute-start(bf16[48,768]{1,0:T(8,128)(2,1)S(1)} %get-tuple-element.33), channel_id=1, source_target_pairs={{0,12},{2,14},{4,8},{6,10},{8,4},{10,6},{12,0},{14,2},{1,13},{3,15... | collective-permute-start | bytes 221192 | tf_op jit(solution)/shard_map/ppermute | solution.py:19
  39.4 6.9 %collective-permute-start.2 = (bf16[48,768]{1,0:T(8,128)(2,1)}, bf16[48,768]{1,0:T(8,128)(2,1)S(1)}, u32[]{:S(2)}, u32[]{:S(2)}) collective-permute-start(bf16[48,768]{1,0:T(8,128)(2,1)} %get-tuple-element.26), channel_id=1, source_target_pairs={{0,8},{2,10},{4,12},{6,14},{8,0},{10,2},{12,4},{14,6},{1,9},{3,11}... | collective-permute-start | bytes 221192 | tf_op jit(solution)/shard_map/ppermute | solution.py:19
  44.0 6.4 %collective-permute-start.3 = (bf16[48,768]{1,0:T(8,128)(2,1)}, bf16[48,768]{1,0:T(8,128)(2,1)S(1)}, u32[]{:S(2)}, u32[]{:S(2)}) collective-permute-start(bf16[48,768]{1,0:T(8,128)(2,1)} %get-tuple-element.27), channel_id=1, source_target_pairs={{0,12},{2,14},{4,8},{6,10},{8,4},{10,6},{12,0},{14,2},{1,13},{3,15... | collective-permute-start | bytes 221192 | tf_op jit(solution)/shard_map/ppermute | solution.py:19
  51.3 12.4 %collective-permute-start.12 = (bf16[3,48,768]{2,1,0:T(8,128)(2,1)S(1)}, bf16[3,48,768]{2,1,0:T(8,128)(2,1)S(1)}, u32[]{:S(2)}, u32[]{:S(2)}) collective-permute-start(bf16[3,48,768]{2,1,0:T(8,128)(2,1)S(1)} %get-tuple-element.41.rounded_ref), channel_id=1, source_target_pairs={{0,1},{1,0},{2,3},{3,2},{4,5},{5,4},{6,7},{7,6},{8,9},{9,8},{10,11... | collective-permute-start | bytes 663560 | tf_op jit(solution)/shard_map/ppermute | solution.py:19
  51.3 9.3 %collective-permute-start.14 = (bf16[48,768]{1,0:T(8,128)(2,1)S(1)}, bf16[48,768]{1,0:T(8,128)(2,1)S(1)}, u32[]{:S(2)}, u32[]{:S(2)}) collective-permute-start(bf16[48,768]{1,0:T(8,128)(2,1)S(1)} %shard_map.76), channel_id=1, source_target_pairs={{0,8},{2,10},{4,12},{6,14},{8,0},{10,2},{12,4},{14,6},{1,9},{3,11}... | collective-permute-start | bytes 221192 | tf_op jit(solution)/shard_map/ppermute | solution.py:19
  51.4 10.7 %collective-permute-start.15 = (bf16[48,768]{1,0:T(8,128)(2,1)S(1)}, bf16[48,768]{1,0:T(8,128)(2,1)S(1)}, u32[]{:S(2)}, u32[]{:S(2)}) collective-permute-start(bf16[48,768]{1,0:T(8,128)(2,1)S(1)} %shard_map.77), channel_id=1, source_target_pairs={{0,8},{2,10},{4,12},{6,14},{8,0},{10,2},{12,4},{14,6},{1,9},{3,11}... | collective-permute-start | bytes 221192 | tf_op jit(solution)/shard_map/ppermute | solution.py:19
  54.4 9.2 %collective-permute-start.13 = (bf16[48,768]{1,0:T(8,128)(2,1)S(1)}, bf16[48,768]{1,0:T(8,128)(2,1)S(1)}, u32[]{:S(2)}, u32[]{:S(2)}) collective-permute-start(bf16[48,768]{1,0:T(8,128)(2,1)S(1)} %shard_map.75), channel_id=1, source_target_pairs={{0,8},{2,10},{4,12},{6,14},{8,0},{10,2},{12,4},{14,6},{1,9},{3,11}... | collective-permute-start | bytes 221192 | tf_op jit(solution)/shard_map/ppermute | solution.py:19
  64.4 3.8 %collective-permute-start.16 = (f32[3,768]{1,0:T(4,128)S(1)}, f32[3,768]{1,0:T(4,128)S(1)}, u32[]{:S(2)}, u32[]{:S(2)}) collective-permute-start(f32[3,768]{1,0:T(4,128)S(1)} %shard_map.78), channel_id=1, source_target_pairs={{0,2},{2,0},{4,6},{6,4},{8,10},{10,8},{12,14},{14,12},{1,3},{3,1},... | collective-permute-start | bytes 27656 | tf_op jit(solution)/shard_map/ppermute | solution.py:19
  68.2 3.7 %collective-permute-start.17 = (f32[3,768]{1,0:T(4,128)S(1)}, f32[3,768]{1,0:T(4,128)S(1)}, u32[]{:S(2)}, u32[]{:S(2)}) collective-permute-start(f32[3,768]{1,0:T(4,128)S(1)} %add.65), channel_id=1, source_target_pairs={{0,4},{2,6},{4,0},{6,2},{8,12},{10,14},{12,8},{14,10},{1,5},{3,7},... | collective-permute-start | bytes 27656 | tf_op jit(solution)/shard_map/ppermute | solution.py:19
  71.9 4.6 %collective-permute-start.18 = (f32[3,768]{1,0:T(4,128)S(1)}, f32[3,768]{1,0:T(4,128)S(1)}, u32[]{:S(2)}, u32[]{:S(2)}) collective-permute-start(f32[3,768]{1,0:T(4,128)S(1)} %add.66), channel_id=1, source_target_pairs={{0,8},{2,10},{4,12},{6,14},{8,0},{10,2},{12,4},{14,6},{1,9},{3,11}... | collective-permute-start | bytes 27656 | tf_op jit(solution)/shard_map/ppermute | solution.py:19
where the time goes:
time: 77.3 us; the launch traced here: 77.1 us
  waiting for transfers between devices  38 us (49%)
  starting transfers between devices  26.9 us (35%)
  Pallas kernels  7.33 us (9%)
  local copies, waits for them, and re-layouts  3.45 us (4%)
    ppermute x19, waiting for transfers between devices, swap(): return lax.ppermute(block, axis, [(i, i ^ mask) for i in range(size)])  38 us
    ppermute x19, starting transfers between devices, swap(): return lax.ppermute(block, axis, [(i, i ^ mask) for i in range(size)])  26.9 us
    pallas_call x11, Pallas kernels, call(): pl.pallas_call(kernel, out_shape=outs, in_specs=[smem] * n_scalar + [vmem...  7.33 us
    unnamed x16, local copies, waits for them, and re-layouts  2.81 us
  transfers between devices with their start and end apart: 19, of which 13 were waited for; matrix products, arithmetic and copies ran while one was open for 1% of the time, Pallas kernels for 7%

commit v1 on v0

--- a/solution.py
+++ b/solution.py
@@ -1,5 +1,6 @@
 import functools
 import math
+from typing import NamedTuple
 
 import jax
 import jax.numpy as jnp
@@ -19,32 +20,78 @@
     return lax.ppermute(block, axis, [(i, i ^ mask) for i in range(size)])
 
 
+class Route(NamedTuple):
+    pair: int
+    near: int
+    over: int
+    halve_phased: bool
+
+    def masks(self):
+        return (0, self.near, self.over, self.near | self.over)
+
+
+def routes(slices):
+    along_x, along_z = Route(1, 2, 4, False), Route(2, 1, 4, True)
+    return [along_z if t % 3 == 1 else along_x for t in range(slices)]
+
+
 PHASE_ROWS = 16
 
 
-def prep_kernel(t, nline, block, owner_ref, phase_ref, w_ref, v_ref, send_ref, own_ref, turned):
-    width = w_ref.shape[2]
+def pack(route, block, owner_ref, w_ref, phase_ref, send_ref, own_ref, turned):
+    width = w_ref.shape[-1]
     nmode = width // 2
     me = lax.axis_index("space")
-    line, side = me // 2, me % 2
+    masks = route.masks()
+    nline = len(masks)
     for c in range(width // LANES):
-        turned[c * LANES : (c + 1) * LANES, :] = w_ref[t, :, c * LANES : (c + 1) * LANES].T
-    for k in range(nline):
-        for half, out_ref in ((1 - side, send_ref), (side, own_ref)):
-            rows = owner_ref[2 * (line ^ k) + half] * block
+        turned[c * LANES : (c + 1) * LANES, :] = w_ref[:, c * LANES : (c + 1) * LANES].T
+    for k, mask in enumerate(masks):
+        for out_ref, whose in ((send_ref, me ^ route.pair), (own_ref, me)):
+            rows = owner_ref[whose ^ mask] * block
             for part in range(2):
                 at = (part * nline + k) * block
                 out_ref[at : at + block, :] = turned[pl.ds(pl.multiple_of(part * nmode + rows, block), block), :]
-    base, sites = 2 * nline * block, v_ref.shape[1]
+    phase = phase_ref[...].astype(jnp.float32).astype(jnp.bfloat16)
+    send_ref[send_ref.shape[0] - PHASE_ROWS :, :] = jnp.broadcast_to(phase, (PHASE_ROWS, LANES))
+
+
+def first_prep_kernel(t, route, block, owner_any, phase_any, w_any, v_any, send_ref, own_ref, turned, w_buf, phase_buf, owner_buf, sems):
+    sites, width = w_buf.shape
+    base = 2 * len(route.masks()) * block
+    copies = [
+        pltpu.make_async_copy(owner_any, owner_buf, sems.at[0]),
+        pltpu.make_async_copy(phase_any, phase_buf, sems.at[1]),
+        pltpu.make_async_copy(w_any.at[t], w_buf, sems.at[2]),
+    ]
+    for c in range(width // LANES):
+        copies.append(
+            pltpu.make_async_copy(
+                v_any.at[t, :, c * LANES : (c + 1) * LANES],
+                send_ref.at[base + c * sites : base + (c + 1) * sites, :],
+                sems.at[3 + c],
+            )
+        )
+    for copy in copies:
+        copy.start()
+    for copy in copies[:3]:
+        copy.wait()
+    pack(route, block, owner_buf, w_buf, phase_buf, send_ref, own_ref, turned)
+    for copy in copies[3:]:
+        copy.wait()
+
+
+def prep_kernel(t, route, block, owner_ref, phase_ref, w_ref, v_ref, send_ref, own_ref, turned):
+    sites, width = v_ref.shape[1:]
+    base = 2 * len(route.masks()) * block
     for c in range(width // LANES):
         send_ref[base + c * sites : base + (c + 1) * sites, :] = v_ref[t, :, c * LANES : (c + 1) * LANES]
-    base += width // LANES * sites
-    phase = phase_ref[...].astype(jnp.float32).astype(jnp.bfloat16)
-    send_ref[base : base + PHASE_ROWS, :] = jnp.broadcast_to(phase, (PHASE_ROWS, LANES))
-
-
-def field_kernel(t, nline, block, scale, phase_ref, v_ref, own_ref, got_ref, *refs):
+    pack(route, block, owner_ref, w_ref.at[t], phase_ref, send_ref, own_ref, turned)
+
+
+def field_kernel(t, route, block, scale, phase_ref, v_ref, own_ref, got_ref, *refs):
     (mine_ref, near_ref), far_refs, (left, phased, plain) = refs[:2], refs[2:-3], refs[-3:]
+    nline = len(route.masks())
     sites, width = v_ref.shape[1:]
     nmode = width // 2
     rows = nline * block
@@ -76,39 +123,43 @@
             phased[top, re], phased[top, im] = pr, pi
             phased[low, re], phased[low, im] = pi, -pr
 
-    def part_of(field, k):
+    def rows_of(field, k):
         return field[k * block : (k + 1) * block]
 
-    field = jnp.dot(left[...], phased[...], preferred_element_type=jnp.float32) * scale
-    mine_ref[0] = part_of(field, 0)
-    near_ref[0] = part_of(field, 1).astype(jnp.bfloat16)
-    for k in range(2, nline):
-        far_refs[k - 2][...] = part_of(field, k).astype(jnp.bfloat16)
-    field = jnp.dot(left[...], plain[...], preferred_element_type=jnp.float32) * scale
-    for k in range(nline):
-        if k % 2 == 0:
-            mine_ref[1 + k // 2] = part_of(field, k)
+    slot = 0
+    for right, halve in ((phased, route.halve_phased), (plain, True)):
+        field = jnp.dot(left[...], right[...], preferred_element_type=jnp.float32) * scale
+        mine_ref[slot] = rows_of(field, 0)
+        near_ref[slot] = rows_of(field, 1).astype(jnp.bfloat16)
+        slot += 1
+        if halve:
+            mine_ref[slot] = rows_of(field, 2)
+            near_ref[slot] = rows_of(field, 3).astype(jnp.bfloat16)
+            slot += 1
         else:
-            near_ref[1 + k // 2] = part_of(field, k).astype(jnp.bfloat16)
-
-
-def cross_kernel(mine_ref, near_ref, out_ref):
-    out_ref[...] = (mine_ref[2] + near_ref[2].astype(jnp.float32)).astype(jnp.bfloat16)
-
-
-def strip_kernel(tdev, *refs):
-    ins, (strip_ref, round_ref) = refs[:-2], refs[-2:]
-    each = len(ins) // tdev
-    for t in range(tdev):
-        mine_ref, near_ref, *far_refs = ins[t * each : (t + 1) * each]
+            for k in (2, 3):
+                far_refs[k - 2][...] = rows_of(field, k).astype(jnp.bfloat16)
+
+
+def cross_kernel(route, mine_ref, near_ref, out_ref):
+    for i, slot in enumerate((1, 3) if route.halve_phased else (2,)):
+        out_ref[i] = (mine_ref[slot] + near_ref[slot].astype(jnp.float32)).astype(jnp.bfloat16)
+
+
+def strip_kernel(plan, *refs):
+    ins, (strip_ref, round_ref) = list(refs[:-2]), refs[-2:]
+    for t, route in enumerate(plan):
+        mine_ref, near_ref = ins.pop(0), ins.pop(0)
         total = mine_ref[0] + near_ref[0].astype(jnp.float32)
-        for far_ref in far_refs:
-            total = total + far_ref[...].astype(jnp.float32)
+        if route.halve_phased:
+            total = total + ins.pop(0)[0].astype(jnp.float32)
+        else:
+            total = total + ins.pop(0)[...].astype(jnp.float32) + ins.pop(0)[...].astype(jnp.float32)
         strip_ref[t] = total
         round_ref[t] = total.astype(jnp.bfloat16)
 
 
-def margin_kernel(tdev, scale, pick_ref, owner_ref, rounded_ref, other_ref, *refs):
+def margin_kernel(plan, scale, pick_ref, owner_ref, rounded_ref, other_ref, *refs):
     ins, out_ref = refs[:-1], refs[-1]
     block, width = rounded_ref.shape[1:]
     nmode = width // 2
@@ -116,9 +167,11 @@
     lane = lax.broadcasted_iota(jnp.int32, (block, nmode), 1)
     row = lax.broadcasted_iota(jnp.int32, (block, nmode), 0)
     here = lane == row + first
-    for t in range(tdev):
+    tdev = len(plan)
+    for t, route in enumerate(plan):
         mine_ref, near_ref, cross_ref = ins[3 * t : 3 * t + 3]
-        total = mine_ref[1] + near_ref[1].astype(jnp.float32) + cross_ref[...].astype(jnp.float32)
+        slot, last = (2, 1) if route.halve_phased else (1, 0)
+        total = mine_ref[slot] + near_ref[slot].astype(jnp.float32) + cross_ref[last].astype(jnp.float32)
         pick = pick_ref[t]
         inside = pick < tdev
         at = jnp.where(inside, pick, pick - tdev)
@@ -144,11 +197,11 @@
     vmem, smem = pl.BlockSpec(memory_space=pltpu.VMEM), pl.BlockSpec(memory_space=pltpu.SMEM)
     shape = jax.ShapeDtypeStruct
 
-    def call(kernel, outs, n_scalar, cost, args, scratch=()):
+    def call(kernel, outs, n_scalar, cost, args, scratch=(), specs=None):
         return pl.pallas_call(
             kernel,
             out_shape=outs,
-            in_specs=[smem] * n_scalar + [vmem] * (len(args) - n_scalar),
+            in_specs=specs or [smem] * n_scalar + [vmem] * (len(args) - n_scalar),
             out_specs=jax.tree.map(lambda _: vmem, outs),
             scratch_shapes=scratch,
             compiler_params=pltpu.CompilerParams(vmem_limit_bytes=GRANT),
@@ -157,38 +210,60 @@
 
     phases = phase_index.reshape(1, sdev)
     packed = 2 * rows + width // LANES * sdev + PHASE_ROWS
+    plan = routes(tdev)
     sends, owns = [], []
-    for t in range(tdev):
+    for t, route in enumerate(plan):
+        first = t == 0
+        scratch = [pltpu.VMEM((width, LANES), bf16)]
+        if first:
+            scratch += [
+                pltpu.VMEM((sdev, width), bf16),
+                pltpu.VMEM((1, sdev), jnp.int32),
+                pltpu.SMEM((nspace,), jnp.int32),
+                pltpu.SemaphoreType.DMA((3 + width // LANES,)),
+            ]
         send, own = call(
-            functools.partial(prep_kernel, t, nline, block),
+            functools.partial(first_prep_kernel if first else prep_kernel, t, route, block),
             (shape((packed, LANES), bf16), shape((2 * rows, LANES), bf16)),
             1,
             4_000_000,
-            (owner_block, phases, w_modes, v_modes),
-            [pltpu.VMEM((width, LANES), bf16)],
+            tuple(pltpu.with_memory_space_constraint(a, pltpu.HBM) for a in (owner_block, phases, w_modes, v_modes))
+            if first
+            else (owner_block, phases, w_modes, v_modes),
+            scratch,
+            [pl.BlockSpec(memory_space=pltpu.HBM)] * 4 if first else None,
         )
         sends.append(send)
         owns.append(own)
-    gots = [swap(send, "space", 1) for send in sends]
+    gots = [swap(send, "space", plan[t].pair) for t, send in enumerate(sends)]
 
     fields, sums = [], []
-    for t in range(tdev):
+    for t, route in enumerate(plan):
+        slots = 4 if route.halve_phased else 3
         mine, near, *fars = call(
-            functools.partial(field_kernel, t, nline, block, scale_sites),
-            [shape((3, block, width), f32), shape((3, block, width), bf16)] + [shape((block, width), bf16)] * (nline - 2),
+            functools.partial(field_kernel, t, route, block, scale_sites),
+            [shape((slots, block, width), f32), shape((slots, block, width), bf16)]
+            + [shape((block, width), bf16)] * (0 if route.halve_phased else 2),
             0,
             4 * rows * 4 * sdev * width,
             (phases, v_modes, owns[t], gots[t]),
             [pltpu.VMEM((rows, 4 * sdev), bf16)] + [pltpu.VMEM((4 * sdev, width), bf16)] * 2,
         )
-        near = swap(near, "space", 2)
-        fars = [swap(far, "space", 2 * k) for k, far in enumerate(fars, 2)]
-        cross = call(cross_kernel, shape((block, width), bf16), 0, 1_000_000, (mine, near))
-        fields.extend([mine, near, *fars])
-        sums.extend([mine, near, swap(cross, "space", 4)])
+        near = swap(near, "space", route.near)
+        fars = [swap(far, "space", route.masks()[k]) for k, far in enumerate(fars, 2)]
+        cross = call(
+            functools.partial(cross_kernel, route),
+            shape((2 if route.halve_phased else 1, block, width), bf16),
+            0,
+            1_000_000,
+            (mine, near),
+        )
+        cross = swap(cross, "space", route.over)
+        fields.extend([mine, near] + (fars or [cross]))
+        sums.extend([mine, near, cross])
 
     strips, rounded = call(
-        functools.partial(strip_kernel, tdev),
+        functools.partial(strip_kernel, plan),
         (shape((tdev, block, width), f32), shape((tdev, block, width), bf16)),
         0,
         1_000_000,
@@ -201,7 +276,7 @@
     target = (global_slice + jnp.take(seq_offset, global_slice)) % total_slices
     pick = (target - rank * tdev) % total_slices
     margin = call(
-        functools.partial(margin_kernel, tdev, scale_modes),
+        functools.partial(margin_kernel, plan, scale_modes),
         shape((tdev, width), f32),
         2,
         1_000_000,

time: 77.3 us -> 71.1 us (0.920)
  starting transfers between devices: 26.9 us -> 24 us
  waiting for transfers between devices: 38 us -> 35.1 us
    ppermute x19 -> x17, starting transfers between devices: 26.9 us -> 24 us  [swap(): return lax.ppermute(block, axis, [(i, i ^ mask) for i in range(size)])]
    ppermute x19 -> x17, waiting for transfers between devices: 38 us -> 35.1 us  [swap(): return lax.ppermute(block, axis, [(i, i ^ mask) for i in range(size)])]
    unnamed x16 -> x18, local copies, waits for them, and re-layouts: 2.81 us -> 2.82 us
  transfers between devices with their start and end apart: 19 -> 17, of which waited for: 13 -> 11; matrix products, arithmetic and copies ran while one was open for 1% -> 1% of each run, Pallas kernels for 7% -> 8%
where the time goes in v1:
time: 71.1 us; the launch traced here: 70.8 us
  waiting for transfers between devices  35.1 us (49%)
  starting transfers between devices  24 us (34%)
  Pallas kernels  6.77 us (10%)
  local copies, waits for them, and re-layouts  3.46 us (5%)
  between operations  0.77 us (1%)
    ppermute x17, waiting for transfers between devices, swap(): return lax.ppermute(block, axis, [(i, i ^ mask) for i in range(size)])  35.1 us
    ppermute x17, starting transfers between devices, swap(): return lax.ppermute(block, axis, [(i, i ^ mask) for i in range(size)])  24 us
    pallas_call x11, Pallas kernels, call(): pl.pallas_call(kernel, out_shape=outs, in_specs=specs or [smem] * n_scala...  6.77 us
    unnamed x18, local copies, waits for them, and re-layouts  2.82 us
  transfers between devices with their start and end apart: 17, of which 11 were waited for; matrix products, arithmetic and copies ran while one was open for 1% of the time, Pallas kernels for 8%

profile of v1, /device:TPU:0, one launch (start us, length us, event | category | flops | bytes accessed | tf_op | source)
XLA Modules:
  0.0 70.8 jit_solution(3999201234405749539)
XLA Ops:
  0.6 0.0 copy-start
  0.6 0.0 copy-start.5
  0.7 0.0 copy-start.7
  0.7 0.6 copy-done.5
  1.3 0.0 copy-done.7
  1.3 1.1 %copy-done.1 = bf16[3,128,768]{2,1,0:T(8,128)(2,1)S(1)} copy-done((bf16[3,128,768]{2,1,0:T(8,128)(2,1)S(1)}, bf16[3,128,768]{2,1,0:T(8,128)(2,1)}, u32[]{:S(2)}) %copy-start.1) | copy-done | bytes 589848
  2.4 1.1 %copy-done.3 = bf16[3,128,768]{2,1,0:T(8,128)(2,1)S(1)} copy-done((bf16[3,128,768]{2,1,0:T(8,128)(2,1)S(1)}, bf16[3,128,768]{2,1,0:T(8,128)(2,1)}, u32[]{:S(2)}) %copy-start.3) | copy-done | bytes 589848
  3.5 0.7 shard_map.70
  4.1 0.0 copy-start.2
  4.1 0.0 copy-start.4
  4.1 3.1 %collective-permute-start.4 = (bf16[1168,128]{1,0:T(8,128)(2,1)S(1)}, bf16[1168,128]{1,0:T(8,128)(2,1)S(1)}, u32[]{:S(2)}, u32[]{:S(2)}) collective-permute-start(bf16[1168,128]{1,0:T(8,128)(2,1)S(1)} %get-tuple-element.27), channel_id=1, source_target_pairs={{0,4},{2,6},{4,0},{6,2},{8,12},{10,14},{12,8},{14,10},{1,5},{3,7},... | collective-permute-start | bytes 897032 | tf_op jit(solution)/shard_map/ppermute | solution.py:20
  7.3 1.2 %shard_map.68 = (bf16[1168,128]{1,0:T(8,128)(2,1)S(1)}, bf16[384,128]{1,0:T(8,128)(2,1)S(1)}) custom-call(s32[8]{0:T(128)} %owner_ref.5, s32[1,128]{1,0:T(1,128)} %bitcast.4, bf16[3,128,768]{2,1,0:T(8,128)(2,1)} %w_ref.3, bf16[3,128,768]{2,1,0:T(8,128)(2,1)} %v_ref.9), custom_call_target="tpu_custom_call" | custom-call | flops 4000000 | bytes 1000000 | tf_op jit(solution)/shard_map/pallas_call | solution.py:201
  8.4 0.0 copy-start.6
  8.4 0.0 copy-start.8
  8.4 1.6 %collective-permute-start = (bf16[1168,128]{1,0:T(8,128)(2,1)S(1)}, bf16[1168,128]{1,0:T(8,128)(2,1)S(1)}, u32[]{:S(2)}, u32[]{:S(2)}) collective-permute-start(bf16[1168,128]{1,0:T(8,128)(2,1)S(1)} %get-tuple-element.21), channel_id=1, source_target_pairs={{0,2},{2,0},{4,6},{6,4},{8,10},{10,8},{12,14},{14,12},{1,3},{3,1},... | collective-permute-start | bytes 897032 | tf_op jit(solution)/shard_map/ppermute | solution.py:20
  10.0 0.7 shard_map.73
  10.7 0.6 collective-permute-start.7
  11.3 3.0 %collective-permute-done.4.got_ref = bf16[1168,128]{1,0:T(8,128)(2,1)S(1)} collective-permute-done((bf16[1168,128]{1,0:T(8,128)(2,1)S(1)}, bf16[1168,128]{1,0:T(8,128)(2,1)S(1)}, u32[]{:S(2)}, u32[]{:S(2)}) %collective-permute-start.4) | collective-permute-done | bytes 299040 | tf_op jit(solution)/shard_map/ppermute | solution.py:20
  14.4 0.9 %shard_map.71 = (f32[4,48,768]{2,1,0:T(8,128)S(1)}, bf16[4,48,768]{2,1,0:T(8,128)(2,1)S(1)}) custom-call(s32[1,128]{1,0:T(1,128)S(1)} %bitcast.7, bf16[3,128,768]{2,1,0:T(8,128)(2,1)S(1)} %copy-done.4, bf16[384,128]{1,0:T(8,128)(2,1)S(1)} %get-tuple-element.26.own_ref, bf16[1168,128]{1,0:T(8,128)(2,1)S(1)} %collective-permute-done.4.got_ref), custom_call_target="tpu_custom_call" | custom-call | flops 301989888 | bytes 1000000 | tf_op jit(solution)/shard_map/pallas_call | solution.py:201
  15.2 1.7 %collective-permute-start.5 = (bf16[4,48,768]{2,1,0:T(8,128)(2,1)S(1)}, bf16[4,48,768]{2,1,0:T(8,128)(2,1)S(1)}, u32[]{:S(2)}, u32[]{:S(2)}) collective-permute-start(bf16[4,48,768]{2,1,0:T(8,128)(2,1)S(1)} %get-tuple-element.29), channel_id=1, source_target_pairs={{0,2},{2,0},{4,6},{6,4},{8,10},{10,8},{12,14},{14,12},{1,3},{3,1},... | collective-permute-start | bytes 884744 | tf_op jit(solution)/shard_map/ppermute | solution.py:20
  16.9 1.5 %collective-permute-done.got_ref = bf16[1168,128]{1,0:T(8,128)(2,1)S(1)} collective-permute-done((bf16[1168,128]{1,0:T(8,128)(2,1)S(1)}, bf16[1168,128]{1,0:T(8,128)(2,1)S(1)}, u32[]{:S(2)}, u32[]{:S(2)}) %collective-permute-start) | collective-permute-done | bytes 299040 | tf_op jit(solution)/shard_map/ppermute | solution.py:20
  18.5 0.9 %shard_map.69 = (f32[3,48,768]{2,1,0:T(8,128)S(1)}, bf16[3,48,768]{2,1,0:T(8,128)(2,1)S(1)}, bf16[48,768]{1,0:T(8,128)(2,1)S(1)}, bf16[48,768]{1,0:T(8,128)(2,1)S(1)}) custom-call(s32[1,128]{1,0:T(1,128)S(1)} %bitcast.8, bf16[3,128,768]{2,1,0:T(8,128)(2,1)S(1)} %copy-done.4, bf16[384,128]{1,0:T(8,128)(2,1)S(1)} %get-tuple-element.20.own_ref, ...), custom_call_target="tpu_custom_call" | custom-call | flops 301989888 | bytes 1000000 | tf_op jit(solution)/shard_map/pallas_call | solution.py:201
  19.3 0.2 collective-permute-start.1
  19.5 5.4 %collective-permute-done.7.got_ref = bf16[1168,128]{1,0:T(8,128)(2,1)S(1)} collective-permute-done((bf16[1168,128]{1,0:T(8,128)(2,1)S(1)}, bf16[1168,128]{1,0:T(8,128)(2,1)S(1)}, u32[]{:S(2)}, u32[]{:S(2)}) %collective-permute-start.7) | collective-permute-done | bytes 299040 | tf_op jit(solution)/shard_map/ppermute | solution.py:20
  24.9 0.9 %shard_map.74 = (f32[3,48,768]{2,1,0:T(8,128)S(1)}, bf16[3,48,768]{2,1,0:T(8,128)(2,1)S(1)}, bf16[48,768]{1,0:T(8,128)(2,1)S(1)}, bf16[48,768]{1,0:T(8,128)(2,1)S(1)}) custom-call(s32[1,128]{1,0:T(1,128)S(1)} %bitcast.9, bf16[3,128,768]{2,1,0:T(8,128)(2,1)S(1)} %copy-done.4, bf16[384,128]{1,0:T(8,128)(2,1)S(1)} %get-tuple-element.30.own_ref, ...), custom_call_target="tpu_custom_call" | custom-call | flops 301989888 | bytes 1000000 | tf_op jit(solution)/shard_map/pallas_call | solution.py:201
  25.8 0.2 collective-permute-start.8
  25.9 3.9 %collective-permute-done.5.near_ref.refs_5_.refs_4_ = bf16[4,48,768]{2,1,0:T(8,128)(2,1)S(1)} collective-permute-done((bf16[4,48,768]{2,1,0:T(8,128)(2,1)S(1)}, bf16[4,48,768]{2,1,0:T(8,128)(2,1)S(1)}, u32[]{:S(2)}, u32[]{:S(2)}) %collective-permute-start.5) | collective-permute-done | bytes 294944 | tf_op jit(solution)/shard_map/ppermute | solution.py:20
  29.8 2.7 %collective-permute-start.6 = (bf16[2,48,768]{2,1,0:T(8,128)(2,1)S(1)}, bf16[2,48,768]{2,1,0:T(8,128)(2,1)S(1)}, u32[]{:S(2)}, u32[]{:S(2)}) collective-permute-start(bf16[2,48,768]{2,1,0:T(8,128)(2,1)S(1)} %shard_map.72), channel_id=1, source_target_pairs={{0,8},{2,10},{4,12},{6,14},{8,0},{10,2},{12,4},{14,6},{1,9},{3,11}... | collective-permute-start | bytes 442376 | tf_op jit(solution)/shard_map/ppermute | solution.py:20
  32.5 0.3 collective-permute-start.2
  32.8 2.6 %collective-permute-start.3 = (bf16[48,768]{1,0:T(8,128)(2,1)S(1)}, bf16[48,768]{1,0:T(8,128)(2,1)S(1)}, u32[]{:S(2)}, u32[]{:S(2)}) collective-permute-start(bf16[48,768]{1,0:T(8,128)(2,1)S(1)} %get-tuple-element.25), channel_id=1, source_target_pairs={{0,12},{2,14},{4,8},{6,10},{8,4},{10,6},{12,0},{14,2},{1,13},{3,15... | collective-permute-start | bytes 221192 | tf_op jit(solution)/shard_map/ppermute | solution.py:20
  35.4 0.0 collective-permute-start.9
  35.4 2.9 %collective-permute-start.10 = (bf16[48,768]{1,0:T(8,128)(2,1)S(1)}, bf16[48,768]{1,0:T(8,128)(2,1)S(1)}, u32[]{:S(2)}, u32[]{:S(2)}) collective-permute-start(bf16[48,768]{1,0:T(8,128)(2,1)S(1)} %get-tuple-element.35), channel_id=1, source_target_pairs={{0,12},{2,14},{4,8},{6,10},{8,4},{10,6},{12,0},{14,2},{1,13},{3,15... | collective-permute-start | bytes 221192 | tf_op jit(solution)/shard_map/ppermute | solution.py:20
  38.4 0.6 gather_fusion
  39.0 8.4 %collective-permute-done.2.refs_2_ = bf16[48,768]{1,0:T(8,128)(2,1)S(1)} collective-permute-done((bf16[48,768]{1,0:T(8,128)(2,1)S(1)}, bf16[48,768]{1,0:T(8,128)(2,1)S(1)}, u32[]{:S(2)}, u32[]{:S(2)}) %collective-permute-start.2) | collective-permute-done | bytes 73760 | tf_op jit(solution)/shard_map/ppermute | solution.py:20
  47.5 0.0 collective-permute-start.12
  47.5 3.9 %collective-permute-start.13 = (bf16[1,48,768]{2,1,0:T(8,128)(2,1)S(1)}, bf16[1,48,768]{2,1,0:T(8,128)(2,1)S(1)}, u32[]{:S(2)}, u32[]{:S(2)}) collective-permute-start(bf16[1,48,768]{2,1,0:T(8,128)(2,1)S(1)} %shard_map.77), channel_id=1, source_target_pairs={{0,8},{2,10},{4,12},{6,14},{8,0},{10,2},{12,4},{14,6},{1,9},{3,11}... | collective-permute-start | bytes 221192 | tf_op jit(solution)/shard_map/ppermute | solution.py:20
  51.4 0.1 collective-permute-done.9.refs_9_
  51.4 0.9 %shard_map.75 = (f32[3,48,768]{2,1,0:T(8,128)}, bf16[3,48,768]{2,1,0:T(8,128)(2,1)S(1)}) custom-call(f32[3,48,768]{2,1,0:T(8,128)S(1)} %get-tuple-element.22.refs_0_.mine_ref, bf16[3,48,768]{2,1,0:T(8,128)(2,1)S(1)} %collective-permute-done.1.refs_1_.near_ref, bf16[48,768]{1,0:T(8,128)(2,1)S(1)} %collective-permute-done.2.refs_2_, ...), custom_call_target="tpu_custom_call" | custom-call | flops 1000000 | bytes 1000000 | tf_op jit(solution)/shard_map/pallas_call | solution.py:201
  52.3 4.2 %collective-permute-done.12.refs_2_ = bf16[1,48,768]{2,1,0:T(8,128)(2,1)S(1)} collective-permute-done((bf16[1,48,768]{2,1,0:T(8,128)(2,1)S(1)}, bf16[1,48,768]{2,1,0:T(8,128)(2,1)S(1)}, u32[]{:S(2)}, u32[]{:S(2)}) %collective-permute-start.12) | collective-permute-done | bytes 73760 | tf_op jit(solution)/shard_map/ppermute | solution.py:20
  56.6 0.8 %collective-permute-done.13.refs_8_ = bf16[1,48,768]{2,1,0:T(8,128)(2,1)S(1)} collective-permute-done((bf16[1,48,768]{2,1,0:T(8,128)(2,1)S(1)}, bf16[1,48,768]{2,1,0:T(8,128)(2,1)S(1)}, u32[]{:S(2)}, u32[]{:S(2)}) %collective-permute-start.13) | collective-permute-done | bytes 73760 | tf_op jit(solution)/shard_map/ppermute | solution.py:20
  57.4 0.8 %shard_map.78 = f32[3,768]{1,0:T(4,128)S(1)} custom-call(s32[3]{0:T(128)S(1)} %and_select_fusion.pick_ref, s32[8]{0:T(128)S(1)} %copy-done.6, bf16[3,48,768]{2,1,0:T(8,128)(2,1)S(1)} %get-tuple-element.37.rounded_ref, bf16[3,48,768]{2,1,0:T(8,128)(2,1)S(1)} %collective-permute-done.11.other_ref, f32[3,48,768]{2,1,0:T(8,128)S(1)} %get-tuple-element.22.refs_0_.mine_ref, ...), custom_call_target="tpu_custom_call" | custom-call | flops 1000000 | bytes 1000000 | tf_op jit(solution)/shard_map/pallas_call | solution.py:201
  58.1 1.6 %collective-permute-start.14 = (f32[3,768]{1,0:T(4,128)S(1)}, f32[3,768]{1,0:T(4,128)S(1)}, u32[]{:S(2)}, u32[]{:S(2)}) collective-permute-start(f32[3,768]{1,0:T(4,128)S(1)} %shard_map.78), channel_id=1, source_target_pairs={{0,2},{2,0},{4,6},{6,4},{8,10},{10,8},{12,14},{14,12},{1,3},{3,1},... | collective-permute-start | bytes 27656 | tf_op jit(solution)/shard_map/ppermute | solution.py:20
  59.7 2.2 %collective-permute-done.14 = f32[3,768]{1,0:T(4,128)S(1)} collective-permute-done((f32[3,768]{1,0:T(4,128)S(1)}, f32[3,768]{1,0:T(4,128)S(1)}, u32[]{:S(2)}, u32[]{:S(2)}) %collective-permute-start.14) | collective-permute-done | bytes 9248 | tf_op jit(solution)/shard_map/ppermute | solution.py:20
  61.9 0.9 %collective-permute-start.15 = (f32[3,768]{1,0:T(4,128)S(1)}, f32[3,768]{1,0:T(4,128)S(1)}, u32[]{:S(2)}, u32[]{:S(2)}) collective-permute-start(f32[3,768]{1,0:T(4,128)S(1)} %add.65), channel_id=1, source_target_pairs={{0,4},{2,6},{4,0},{6,2},{8,12},{10,14},{12,8},{14,10},{1,5},{3,7},... | collective-permute-start | bytes 27656 | tf_op jit(solution)/shard_map/ppermute | solution.py:20
  62.8 2.8 %collective-permute-done.15 = f32[3,768]{1,0:T(4,128)S(1)} collective-permute-done((f32[3,768]{1,0:T(4,128)S(1)}, f32[3,768]{1,0:T(4,128)S(1)}, u32[]{:S(2)}, u32[]{:S(2)}) %collective-permute-start.15) | collective-permute-done | bytes 9248 | tf_op jit(solution)/shard_map/ppermute | solution.py:20
  65.6 1.9 %collective-permute-start.16 = (f32[3,768]{1,0:T(4,128)S(1)}, f32[3,768]{1,0:T(4,128)S(1)}, u32[]{:S(2)}, u32[]{:S(2)}) collective-permute-start(f32[3,768]{1,0:T(4,128)S(1)} %add.66), channel_id=1, source_target_pairs={{0,8},{2,10},{4,12},{6,14},{8,0},{10,2},{12,4},{14,6},{1,9},{3,11}... | collective-permute-start | bytes 27656 | tf_op jit(solution)/shard_map/ppermute | solution.py:20
  67.5 2.7 %collective-permute-done.16 = f32[3,768]{1,0:T(4,128)S(1)} collective-permute-done((f32[3,768]{1,0:T(4,128)S(1)}, f32[3,768]{1,0:T(4,128)S(1)}, u32[]{:S(2)}, u32[]{:S(2)}) %collective-permute-start.16) | collective-permute-done | bytes 9248 | tf_op jit(solution)/shard_map/ppermute | solution.py:20
  70.2 0.6 add.67
  (22 shorter events, 0.1 us)
Async XLA Ops:
  0.6 37.7 %copy-start = (s32[6]{0:T(128)S(1)}, s32[6]{0:T(128)}, u32[]{:S(2)}) copy-start(s32[6]{0:T(128)} %param.8) | copy-start | bytes 76
  0.6 0.7 copy-start.5
  0.7 0.7 copy-start.7
  1.3 1.1 %copy-start.1 = (bf16[3,128,768]{2,1,0:T(8,128)(2,1)S(1)}, bf16[3,128,768]{2,1,0:T(8,128)(2,1)}, u32[]{:S(2)}) copy-start(bf16[3,128,768]{2,1,0:T(8,128)(2,1)} %w_ref.3) | copy-start | bytes 1769476
  2.4 1.1 %copy-start.3 = (bf16[3,128,768]{2,1,0:T(8,128)(2,1)S(1)}, bf16[3,128,768]{2,1,0:T(8,128)(2,1)}, u32[]{:S(2)}) copy-start(bf16[3,128,768]{2,1,0:T(8,128)(2,1)} %v_ref.9) | copy-start | bytes 1769476
  4.1 5.9 %copy-start.2 = (bf16[3,128,768]{2,1,0:T(8,128)(2,1)S(1)}, bf16[3,128,768]{2,1,0:T(8,128)(2,1)}, u32[]{:S(2)}) copy-start(bf16[3,128,768]{2,1,0:T(8,128)(2,1)} %w_ref.3) | copy-start | bytes 1769476
  4.1 5.9 %copy-start.4 = (bf16[3,128,768]{2,1,0:T(8,128)(2,1)S(1)}, bf16[3,128,768]{2,1,0:T(8,128)(2,1)}, u32[]{:S(2)}) copy-start(bf16[3,128,768]{2,1,0:T(8,128)(2,1)} %v_ref.9) | copy-start | bytes 1769476
  4.1 10.2 %collective-permute-start.4 = (bf16[1168,128]{1,0:T(8,128)(2,1)S(1)}, bf16[1168,128]{1,0:T(8,128)(2,1)S(1)}, u32[]{:S(2)}, u32[]{:S(2)}) collective-permute-start(bf16[1168,128]{1,0:T(8,128)(2,1)S(1)} %get-tuple-element.27), channel_id=1, source_target_pairs={{0,4},{2,6},{4,0},{6,2},{8,12},{10,14},{12,8},{14,10},{1,5},{3,7},... | collective-permute-start | bytes 897032 | tf_op jit(solution)/shard_map/ppermute | solution.py:20
  8.4 1.6 %copy-start.6 = (s32[8]{0:T(128)S(1)}, s32[8]{0:T(128)}, u32[]{:S(2)}) copy-start(s32[8]{0:T(128)} %owner_ref.5) | copy-start | bytes 100
  8.4 1.6 %copy-start.8 = (s32[128]{0:T(128)S(1)}, s32[128]{0:T(128)}, u32[]{:S(2)}) copy-start(s32[128]{0:T(128)} %param.7) | copy-start | bytes 1540
  8.4 10.0 %collective-permute-start = (bf16[1168,128]{1,0:T(8,128)(2,1)S(1)}, bf16[1168,128]{1,0:T(8,128)(2,1)S(1)}, u32[]{:S(2)}, u32[]{:S(2)}) collective-permute-start(bf16[1168,128]{1,0:T(8,128)(2,1)S(1)} %get-tuple-element.21), channel_id=1, source_target_pairs={{0,2},{2,0},{4,6},{6,4},{8,10},{10,8},{12,14},{14,12},{1,3},{3,1},... | collective-permute-start | bytes 897032 | tf_op jit(solution)/shard_map/ppermute | solution.py:20
  10.7 14.2 %collective-permute-start.7 = (bf16[1168,128]{1,0:T(8,128)(2,1)S(1)}, bf16[1168,128]{1,0:T(8,128)(2,1)S(1)}, u32[]{:S(2)}, u32[]{:S(2)}) collective-permute-start(bf16[1168,128]{1,0:T(8,128)(2,1)S(1)} %get-tuple-element.31), channel_id=1, source_target_pairs={{0,2},{2,0},{4,6},{6,4},{8,10},{10,8},{12,14},{14,12},{1,3},{3,1},... | collective-permute-start | bytes 897032 | tf_op jit(solution)/shard_map/ppermute | solution.py:20
  15.2 14.6 %collective-permute-start.5 = (bf16[4,48,768]{2,1,0:T(8,128)(2,1)S(1)}, bf16[4,48,768]{2,1,0:T(8,128)(2,1)S(1)}, u32[]{:S(2)}, u32[]{:S(2)}) collective-permute-start(bf16[4,48,768]{2,1,0:T(8,128)(2,1)S(1)} %get-tuple-element.29), channel_id=1, source_target_pairs={{0,2},{2,0},{4,6},{6,4},{8,10},{10,8},{12,14},{14,12},{1,3},{3,1},... | collective-permute-start | bytes 884744 | tf_op jit(solution)/shard_map/ppermute | solution.py:20
  19.3 16.0 %collective-permute-start.1 = (bf16[3,48,768]{2,1,0:T(8,128)(2,1)S(1)}, bf16[3,48,768]{2,1,0:T(8,128)(2,1)S(1)}, u32[]{:S(2)}, u32[]{:S(2)}) collective-permute-start(bf16[3,48,768]{2,1,0:T(8,128)(2,1)S(1)} %get-tuple-element.23), channel_id=1, source_target_pairs={{0,4},{2,6},{4,0},{6,2},{8,12},{10,14},{12,8},{14,10},{1,5},{3,7},... | collective-permute-start | bytes 663560 | tf_op jit(solution)/shard_map/ppermute | solution.py:20
  25.8 9.7 %collective-permute-start.8 = (bf16[3,48,768]{2,1,0:T(8,128)(2,1)S(1)}, bf16[3,48,768]{2,1,0:T(8,128)(2,1)S(1)}, u32[]{:S(2)}, u32[]{:S(2)}) collective-permute-start(bf16[3,48,768]{2,1,0:T(8,128)(2,1)S(1)} %get-tuple-element.33), channel_id=1, source_target_pairs={{0,4},{2,6},{4,0},{6,2},{8,12},{10,14},{12,8},{14,10},{1,5},{3,7},... | collective-permute-start | bytes 663560 | tf_op jit(solution)/shard_map/ppermute | solution.py:20
  29.8 21.6 %collective-permute-start.6 = (bf16[2,48,768]{2,1,0:T(8,128)(2,1)S(1)}, bf16[2,48,768]{2,1,0:T(8,128)(2,1)S(1)}, u32[]{:S(2)}, u32[]{:S(2)}) collective-permute-start(bf16[2,48,768]{2,1,0:T(8,128)(2,1)S(1)} %shard_map.72), channel_id=1, source_target_pairs={{0,8},{2,10},{4,12},{6,14},{8,0},{10,2},{12,4},{14,6},{1,9},{3,11}... | collective-permute-start | bytes 442376 | tf_op jit(solution)/shard_map/ppermute | solution.py:20
  32.5 15.0 %collective-permute-start.2 = (bf16[48,768]{1,0:T(8,128)(2,1)S(1)}, bf16[48,768]{1,0:T(8,128)(2,1)S(1)}, u32[]{:S(2)}, u32[]{:S(2)}) collective-permute-start(bf16[48,768]{1,0:T(8,128)(2,1)S(1)} %get-tuple-element.24), channel_id=1, source_target_pairs={{0,8},{2,10},{4,12},{6,14},{8,0},{10,2},{12,4},{14,6},{1,9},{3,11}... | collective-permute-start | bytes 221192 | tf_op jit(solution)/shard_map/ppermute | solution.py:20
  32.8 14.7 %collective-permute-start.3 = (bf16[48,768]{1,0:T(8,128)(2,1)S(1)}, bf16[48,768]{1,0:T(8,128)(2,1)S(1)}, u32[]{:S(2)}, u32[]{:S(2)}) collective-permute-start(bf16[48,768]{1,0:T(8,128)(2,1)S(1)} %get-tuple-element.25), channel_id=1, source_target_pairs={{0,12},{2,14},{4,8},{6,10},{8,4},{10,6},{12,0},{14,2},{1,13},{3,15... | collective-permute-start | bytes 221192 | tf_op jit(solution)/shard_map/ppermute | solution.py:20
  35.4 16.0 %collective-permute-start.9 = (bf16[48,768]{1,0:T(8,128)(2,1)S(1)}, bf16[48,768]{1,0:T(8,128)(2,1)S(1)}, u32[]{:S(2)}, u32[]{:S(2)}) collective-permute-start(bf16[48,768]{1,0:T(8,128)(2,1)S(1)} %get-tuple-element.34), channel_id=1, source_target_pairs={{0,8},{2,10},{4,12},{6,14},{8,0},{10,2},{12,4},{14,6},{1,9},{3,11}... | collective-permute-start | bytes 221192 | tf_op jit(solution)/shard_map/ppermute | solution.py:20
  35.4 16.0 %collective-permute-start.10 = (bf16[48,768]{1,0:T(8,128)(2,1)S(1)}, bf16[48,768]{1,0:T(8,128)(2,1)S(1)}, u32[]{:S(2)}, u32[]{:S(2)}) collective-permute-start(bf16[48,768]{1,0:T(8,128)(2,1)S(1)} %get-tuple-element.35), channel_id=1, source_target_pairs={{0,12},{2,14},{4,8},{6,10},{8,4},{10,6},{12,0},{14,2},{1,13},{3,15... | collective-permute-start | bytes 221192 | tf_op jit(solution)/shard_map/ppermute | solution.py:20
  47.5 9.1 %collective-permute-start.12 = (bf16[1,48,768]{2,1,0:T(8,128)(2,1)S(1)}, bf16[1,48,768]{2,1,0:T(8,128)(2,1)S(1)}, u32[]{:S(2)}, u32[]{:S(2)}) collective-permute-start(bf16[1,48,768]{2,1,0:T(8,128)(2,1)S(1)} %shard_map.76), channel_id=1, source_target_pairs={{0,8},{2,10},{4,12},{6,14},{8,0},{10,2},{12,4},{14,6},{1,9},{3,11}... | collective-permute-start | bytes 221192 | tf_op jit(solution)/shard_map/ppermute | solution.py:20
  47.5 9.9 %collective-permute-start.13 = (bf16[1,48,768]{2,1,0:T(8,128)(2,1)S(1)}, bf16[1,48,768]{2,1,0:T(8,128)(2,1)S(1)}, u32[]{:S(2)}, u32[]{:S(2)}) collective-permute-start(bf16[1,48,768]{2,1,0:T(8,128)(2,1)S(1)} %shard_map.77), channel_id=1, source_target_pairs={{0,8},{2,10},{4,12},{6,14},{8,0},{10,2},{12,4},{14,6},{1,9},{3,11}... | collective-permute-start | bytes 221192 | tf_op jit(solution)/shard_map/ppermute | solution.py:20
  52.3 5.1 %collective-permute-start.11 = (bf16[3,48,768]{2,1,0:T(8,128)(2,1)S(1)}, bf16[3,48,768]{2,1,0:T(8,128)(2,1)S(1)}, u32[]{:S(2)}, u32[]{:S(2)}) collective-permute-start(bf16[3,48,768]{2,1,0:T(8,128)(2,1)S(1)} %get-tuple-element.37.rounded_ref), channel_id=1, source_target_pairs={{0,1},{1,0},{2,3},{3,2},{4,5},{5,4},{6,7},{7,6},{8,9},{9,8},{10,11... | collective-permute-start | bytes 663560 | tf_op jit(solution)/shard_map/ppermute | solution.py:20
  58.1 3.8 %collective-permute-start.14 = (f32[3,768]{1,0:T(4,128)S(1)}, f32[3,768]{1,0:T(4,128)S(1)}, u32[]{:S(2)}, u32[]{:S(2)}) collective-permute-start(f32[3,768]{1,0:T(4,128)S(1)} %shard_map.78), channel_id=1, source_target_pairs={{0,2},{2,0},{4,6},{6,4},{8,10},{10,8},{12,14},{14,12},{1,3},{3,1},... | collective-permute-start | bytes 27656 | tf_op jit(solution)/shard_map/ppermute | solution.py:20
  61.9 3.7 %collective-permute-start.15 = (f32[3,768]{1,0:T(4,128)S(1)}, f32[3,768]{1,0:T(4,128)S(1)}, u32[]{:S(2)}, u32[]{:S(2)}) collective-permute-start(f32[3,768]{1,0:T(4,128)S(1)} %add.65), channel_id=1, source_target_pairs={{0,4},{2,6},{4,0},{6,2},{8,12},{10,14},{12,8},{14,10},{1,5},{3,7},... | collective-permute-start | bytes 27656 | tf_op jit(solution)/shard_map/ppermute | solution.py:20
  65.6 4.6 %collective-permute-start.16 = (f32[3,768]{1,0:T(4,128)S(1)}, f32[3,768]{1,0:T(4,128)S(1)}, u32[]{:S(2)}, u32[]{:S(2)}) collective-permute-start(f32[3,768]{1,0:T(4,128)S(1)} %add.66), channel_id=1, source_target_pairs={{0,8},{2,10},{4,12},{6,14},{8,0},{10,2},{12,4},{14,6},{1,9},{3,11}... | collective-permute-start | bytes 27656 | tf_op jit(solution)/shard_map/ppermute | solution.py:20
